TPU v7x, 32 devices: a whole 2x2x4 slice. The times are simulated.
32 devices in a mesh: node: 4 (over z), grp: 2 (over y), rep: 4 (over x, core).
Axes of the slice: x: 2, y: 2, z: 4, core: 2. Of those that a mesh axis runs over, the one named last changes fastest.
Arguments:
- tokens: bfloat16 [1024, 768], P(('node', 'grp'), 'rep'), may hold values from -6 to 6
- gates: float32 [1024, 2], P(('node', 'grp')), may hold values from 0.05 to 1
- expert_ids: int32 [1024, 2], P(('node', 'grp')), may hold values from 0 to 7, all different within a row; in each aligned block of 128 rows (0 to 127, 128 to 255, ...) at most 64 rows name the same one
- w_in: bfloat16 [8, 768, 1536], P(('node', 'grp'), None, 'rep'), may hold values from -0.21875 to 0.21875
- b_in: float32 [8, 1536], P(('node', 'grp'), 'rep'), may hold values from -3 to 3
- w_out: bfloat16 [8, 1536, 768], P(('node', 'grp'), 'rep'), may hold values from -0.15625 to 0.15625
- b_out: float32 [8, 768], P(('node', 'grp'), 'rep'), may hold values from -3 to 3
- cotangent: bfloat16 [1024, 768], P(('node', 'grp'), 'rep'), may hold values from -6 to 6
Outputs:
- mixed: bfloat16 [1024, 768], P(('node', 'grp'), 'rep')
- d_tokens: bfloat16 [1024, 768], P(('node', 'grp'), 'rep')
- d_gates: float32 [1024, 2], P(('node', 'grp'))
- d_w_in: float32 [8, 768, 1536], P(('node', 'grp'), None, 'rep')
- d_b_in: float32 [8, 1536], P(('node', 'grp'), 'rep')
- d_w_out: float32 [8, 1536, 768], P(('node', 'grp'), 'rep')
- d_b_out: float32 [8, 768], P(('node', 'grp'), 'rep')
Inputs may be any that keep to these rules, and one draw needn't show every extreme that they name: `expert_ids`: each row names 2 different experts. Among the 128 rows of one device's aligned block no expert is named more than 64 times, and in some blocks one expert is named exactly 64 times.
All inputs are finite; a program needn't handle non-finite values.
Results may differ from a plain program's by a relative error of at most 0.0064.
Values may be sent and summed in bfloat16 or wider, within the bound.
No kernel may reach another device: no remote copies, remote signals or barrier semaphores. Data moves between devices by JAX's collectives and lax.ppermute only.
A program may use at most 64 MiB of HBM per device.

v0:
```python
import jax
import jax.numpy as jnp
from jax import lax
from jax.sharding import PartitionSpec as P


def contract_first(left, right):
    return lax.dot_general(
        left, right, (((0,), (0,)), ((), ())), preferred_element_type=jnp.float32
    )


def contract_last(left, right):
    return lax.dot_general(
        left, right, (((1,), (1,)), ((), ())), preferred_element_type=jnp.float32
    )


def relocate(buffer):
    return lax.all_to_all(buffer, ("node", "grp"), split_axis=0, concat_axis=0, tiled=True)


def per_device(tokens, gates, expert_ids, w_in, b_in, w_out, b_out, cotangent):
    n_experts = lax.axis_size(("node", "grp"))
    tok_rows, feat_width = tokens.shape
    top_k = expert_ids.shape[1]
    assigned = tok_rows * top_k
    capacity = max(2, 2 * assigned // n_experts)
    rows_total = n_experts * capacity
    flat_ids = expert_ids.reshape(assigned)
    position = jnp.arange(assigned, dtype=jnp.int32)
    matches = (flat_ids[:, None] == flat_ids[None, :]) & (position[None, :] < position[:, None])
    slot_rank = jnp.sum(matches.astype(jnp.int32), axis=1)
    target = flat_ids * capacity + slot_rank
    placing = (jnp.arange(rows_total, dtype=jnp.int32)[:, None] == target[None, :]).astype(
        jnp.bfloat16
    )
    token_copies = jnp.repeat(tokens, top_k, axis=0)
    outbound = jnp.dot(placing, token_copies, preferred_element_type=jnp.float32).astype(
        jnp.bfloat16
    )
    inbound = relocate(outbound.reshape(n_experts, capacity, feat_width))
    expert_x = inbound.reshape(rows_total, feat_width)
    w_first = w_in[0]
    bias_first = b_in[0]
    w_second = w_out[0]
    bias_second = b_out[0]
    feat_local = w_second.shape[1] // lax.axis_size("rep")
    full_x = lax.all_gather(expert_x, "rep", axis=1, tiled=True)
    pre_act = jnp.dot(full_x, w_first, preferred_element_type=jnp.float32)
    pre_act = pre_act + bias_first
    hidden = jax.nn.gelu(pre_act).astype(jnp.bfloat16)
    second_block = lax.all_to_all(w_second, "rep", split_axis=1, concat_axis=0, tiled=True)
    weights = second_block
    summed = jnp.dot(
        lax.all_gather(hidden, "rep", axis=1, tiled=True),
        weights,
        preferred_element_type=jnp.float32,
    )
    expert_out = (summed + bias_second).astype(jnp.bfloat16)
    returned = relocate(expert_out.reshape(n_experts, capacity, feat_local)).reshape(
        rows_total, feat_local
    )
    per_assign = contract_first(placing, returned).reshape(tok_rows, top_k, feat_local)
    mixed = jnp.sum(gates[:, :, None] * per_assign, axis=1).astype(jnp.bfloat16)
    cot_wide = cotangent.astype(jnp.float32)
    gate_terms = jnp.sum(cot_wide[:, None, :] * per_assign, axis=2)
    d_gates = lax.psum(gate_terms, "rep")
    d_out = (
        (gates[:, :, None] * cot_wide[:, None, :])
        .astype(jnp.bfloat16)
        .reshape(assigned, feat_width)
    )
    grad_outbound = jnp.dot(placing, d_out, preferred_element_type=jnp.float32).astype(jnp.bfloat16)
    expert_grad = relocate(grad_outbound.reshape(n_experts, capacity, feat_width)).reshape(
        rows_total, feat_width
    )
    grad_bias_out = jnp.sum(expert_grad.astype(jnp.float32), axis=0)
    full_grad = lax.all_gather(expert_grad, "rep", axis=1, tiled=True)
    grad_w_out = contract_first(hidden, full_grad)
    d_hidden = contract_last(full_grad, w_second)
    _, pull_back = jax.vjp(jax.nn.gelu, pre_act)
    d_pre = pull_back(d_hidden)[0].astype(jnp.bfloat16)
    grad_bias_in = jnp.sum(d_pre.astype(jnp.float32), axis=0)
    grad_w_in = contract_first(full_x, d_pre)
    first_block = lax.all_to_all(w_first, "rep", split_axis=0, concat_axis=1, tiled=True)
    weights = first_block
    row_sums = contract_last(lax.all_gather(d_pre, "rep", axis=1, tiled=True), weights)
    d_rows = row_sums.astype(jnp.bfloat16)
    back_rows = relocate(d_rows.reshape(n_experts, capacity, feat_local)).reshape(
        rows_total, feat_local
    )
    row_grads = contract_first(placing, back_rows).reshape(tok_rows, top_k, feat_local)
    d_tokens = jnp.sum(row_grads, axis=1).astype(jnp.bfloat16)
    return (
        mixed,
        d_tokens,
        d_gates,
        grad_w_in[None],
        grad_bias_in[None],
        grad_w_out[None],
        grad_bias_out[None],
    )


def solution(mesh):
    return jax.shard_map(
        per_device,
        mesh=mesh,
        in_specs=(
            P(("node", "grp"), "rep"),
            P(("node", "grp"), None),
            P(("node", "grp"), None),
            P(("node", "grp"), None, "rep"),
            P(("node", "grp"), "rep"),
            P(("node", "grp"), "rep", None),
            P(("node", "grp"), "rep"),
            P(("node", "grp"), "rep"),
        ),
        out_specs=(
            P(("node", "grp"), "rep"),
            P(("node", "grp"), "rep"),
            P(("node", "grp"), None),
            P(("node", "grp"), None, "rep"),
            P(("node", "grp"), "rep"),
            P(("node", "grp"), "rep", None),
            P(("node", "grp"), "rep"),
        ),
        check_vma=False,
    )
```

profile of v0, /device:TPU:0, one launch (start us, length us, event | category | flops | bytes accessed | tf_op | source)
XLA Modules:
  0.0 130.0 jit_solution(18391526775065766837)
XLA Ops:
  7.2 0.9 copy.49
  8.1 0.1 broadcast_in_dim.10
  8.2 0.1 reshape.108
  8.3 0.8 copy.48
  9.1 0.1 reshape.107
  9.3 0.2 convert_reduce_fusion.2
  9.5 0.3 convolution_convert_fusion.2
  9.8 0.8 copy.50
  10.6 7.3 %all-to-all-start = ((bf16[8,64,192]{2,1,0:T(8,128)(2,1)}), bf16[8,64,192]{2,1,0:T(8,128)(2,1)S(1)}, u32[]{:S(2)}, u32[]{:S(2)}) async-start(bf16[8,64,192]{2,1,0:T(8,128)(2,1)} %bitcast), calls=%async_computation | async-start | bytes 524288 | tf_op jit(solution)/shard_map/all_to_all | solution.py:20
  18.0 8.8 %all-to-all-done = bf16[8,64,192]{2,1,0:T(8,128)(2,1)S(1)} async-done(((bf16[8,64,192]{2,1,0:T(8,128)(2,1)}), bf16[8,64,192]{2,1,0:T(8,128)(2,1)S(1)}, u32[]{:S(2)}, u32[]{:S(2)}) %all-to-all-start) | async-done | bytes 196640 | tf_op jit(solution)/shard_map/all_to_all | solution.py:20
  26.8 0.1 copy.51
  27.0 8.6 %all_gather.12 = bf16[512,768]{0,1:T(8,128)(2,1)S(1)} all-gather(bf16[512,192]{0,1:T(8,128)(2,1)S(1)} %copy.51), channel_id=1, replica_groups=mesh['node'=4,'grp'=2,'rep'=4] {'rep'}, dimensions={1}, use_global_device_ids=true | all-gather | bytes 983040 | tf_op jit(solution)/shard_map/all_gather | solution.py:49
  35.6 1.8 %multiply_convert_fusion = (bf16[512,384]{1,0:T(8,128)(2,1)}, f32[512,384]{1,0:T(8,128)}) fusion(f32[384]{0:T(512)S(1)} %reduce.1, bf16[512,768]{0,1:T(8,128)(2,1)S(1)} %all_gather.12, bf16[1,768,384]{2,1,0:T(8,128)(2,1)S(1)} %copy-done.3), kind=kOutput, calls=%fused_computation.19 | convolution fusion | flops 303955968 | bytes 2557440 | tf_op jit(solution)/shard_map/dot_general | solution.py:50
  37.3 0.0 all-gather.5.cloned.1.call-start
  37.4 0.1 copy.57
  37.5 0.1 mul.97
  37.7 0.1 copy.69
  37.8 0.1 mul.99.clone
  37.9 0.2 mul.100
  38.1 0.3 convolution_convert_fusion.1
  38.4 0.1 copy.59
  38.5 12.8 %all_to_all.58 = bf16[8,64,192]{2,1,0:T(8,128)(2,1)S(1)} all-to-all(bf16[8,64,192]{2,1,0:T(8,128)(2,1)S(1)} %bitcast.55), channel_id=1, replica_groups=mesh['node'=4,'grp'=2,'rep'=4] {'node','grp'}, dimensions={0} | all-to-all | bytes 393216 | tf_op jit(solution)/shard_map/all_to_all | solution.py:20
  51.4 0.1 copy.60
  51.5 7.8 %all_gather.14 = bf16[512,768]{0,1:T(8,128)(2,1)S(1)} all-gather(bf16[512,192]{0,1:T(8,128)(2,1)S(1)} %copy.60), channel_id=1, replica_groups=mesh['node'=4,'grp'=2,'rep'=4] {'rep'}, dimensions={1}, use_global_device_ids=true | all-gather | bytes 983040 | tf_op jit(solution)/shard_map/all_gather | solution.py:79
  59.3 2.9 %convert_reduce_fusion = (f32[384]{0:T(512)S(1)}, bf16[512,384]{1,0:T(8,128)(2,1)}) fusion(f32[512,384]{1,0:T(8,128)} %get-tuple-element.10, bf16[512,768]{0,1:T(8,128)(2,1)S(1)} %all_gather.14, bf16[1,384,768]{2,1,0:T(8,128)(2,1)S(1)} %copy-done.2), kind=kOutput, calls=%fused_computation.18 | convolution fusion | flops 306314880 | bytes 2557440 | tf_op jit(solution)/shard_map/dot_general | solution.py:14
  62.2 1.1 copy.52
  63.3 3.5 %all-to-all-start.1 = ((bf16[384,4,192]{0,2,1:T(8,128)(2,1)}), bf16[384,4,192]{0,2,1:T(8,128)(2,1)S(1)}, u32[]{:S(2)}, u32[]{:S(2)}) async-start(bf16[384,4,192]{0,2,1:T(8,128)(2,1)} %bitcast.3), calls=%async_computation.1 | async-start | bytes 1179648 | tf_op jit(solution)/shard_map/all_to_all | solution.py:53
  66.8 14.5 %all-to-all-done.1 = bf16[384,4,192]{0,2,1:T(8,128)(2,1)S(1)} async-done(((bf16[384,4,192]{0,2,1:T(8,128)(2,1)}), bf16[384,4,192]{0,2,1:T(8,128)(2,1)S(1)}, u32[]{:S(2)}, u32[]{:S(2)}) %all-to-all-start.1) | async-done | bytes 589856 | tf_op jit(solution)/shard_map/all_to_all | solution.py:53
  81.3 3.5 %all-to-all-start.4 = ((bf16[4,192,384]{2,1,0:T(8,128)(2,1)}), bf16[4,192,384]{2,1,0:T(8,128)(2,1)S(1)}, u32[]{:S(2)}, u32[]{:S(2)}) async-start(bf16[4,192,384]{2,1,0:T(8,128)(2,1)} %bitcast.56), calls=%async_computation.4 | async-start | bytes 1179648 | tf_op jit(solution)/shard_map/all_to_all | solution.py:86
  84.8 0.1 iota_compare_fusion.3
  84.9 0.2 eq.50
  85.1 0.9 copy.70
  86.0 2.2 %fusion = bf16[512,192]{0,1:T(8,128)(2,1)S(1)} fusion(bf16[512,1536]{1,0:T(8,128)(2,1)} %all-gather.3.cloned.1.call-done, bf16[1536,192]{0,1:T(8,128)(2,1)} %bitcast.58, f32[192]{0:T(256)S(1)} %bitcast.61), kind=kOutput, calls=%fused_computation.5 | convolution fusion | flops 302186496 | bytes 2360064 | tf_op jit(solution)/shard_map/dot_general | solution.py:55
  88.2 0.8 copy.54
  89.1 5.2 %all-to-all-done.4 = bf16[4,192,384]{2,1,0:T(8,128)(2,1)S(1)} async-done(((bf16[4,192,384]{2,1,0:T(8,128)(2,1)}), bf16[4,192,384]{2,1,0:T(8,128)(2,1)S(1)}, u32[]{:S(2)}, u32[]{:S(2)}) %all-to-all-start.4) | async-done | bytes 589856 | tf_op jit(solution)/shard_map/all_to_all | solution.py:86
  94.3 4.8 %all-to-all-start.2 = ((bf16[8,64,192]{2,1,0:T(8,128)(2,1)}), bf16[8,64,192]{2,1,0:T(8,128)(2,1)}, u32[]{:S(2)}, u32[]{:S(2)}) async-start(bf16[8,64,192]{2,1,0:T(8,128)(2,1)} %bitcast.6), calls=%async_computation.2 | async-start | bytes 524288 | tf_op jit(solution)/shard_map/all_to_all | solution.py:20
  99.1 1.6 %convolution_bitcast_fusion.1 = f32[1,768,384]{2,1,0:T(8,128)} fusion(bf16[512,768]{0,1:T(8,128)(2,1)S(1)} %all_gather.12, bf16[512,384]{1,0:T(8,128)(2,1)S(1)} %copy-done.1), kind=kOutput, calls=%fused_computation.1 | convolution fusion | flops 301989888 | bytes 2359296 | tf_op jit(solution)/shard_map/dot_general | solution.py:8
  100.6 0.1 copy.71
  100.7 2.1 %convolution_convert_fusion = bf16[512,192]{0,1:T(8,128)(2,1)S(1)} fusion(bf16[512,1536]{1,0:T(8,128)(2,1)} %all-gather.5.cloned.1.call-done, bf16[192,1536]{1,0:T(8,128)(2,1)S(1)} %bitcast.57), kind=kOutput, calls=%fused_computation.4 | convolution fusion | flops 302088192 | bytes 2359296 | tf_op jit(solution)/shard_map/dot_general | solution.py:14
  102.9 0.8 copy.62
  103.7 4.1 %all-to-all-done.2 = bf16[8,64,192]{2,1,0:T(8,128)(2,1)} async-done(((bf16[8,64,192]{2,1,0:T(8,128)(2,1)}), bf16[8,64,192]{2,1,0:T(8,128)(2,1)}, u32[]{:S(2)}, u32[]{:S(2)}) %all-to-all-start.2) | async-done | bytes 196640 | tf_op jit(solution)/shard_map/all_to_all | solution.py:20
  107.8 3.6 %all-to-all-start.5 = ((bf16[8,64,192]{2,1,0:T(8,128)(2,1)}), bf16[8,64,192]{2,1,0:T(8,128)(2,1)S(1)}, u32[]{:S(2)}, u32[]{:S(2)}) async-start(bf16[8,64,192]{2,1,0:T(8,128)(2,1)} %bitcast.14), calls=%async_computation.5 | async-start | bytes 524288 | tf_op jit(solution)/shard_map/all_to_all | solution.py:20
  111.4 0.7 convert_reduce_fusion.1
  112.0 0.6 broadcast_in_dim.12
  112.6 1.5 %convolution_bitcast_fusion = f32[1,384,768]{2,1,0:T(8,128)} fusion(bf16[512,384]{1,0:T(8,128)(2,1)S(1)} %copy-done, bf16[512,768]{0,1:T(8,128)(2,1)S(1)} %all_gather.14), kind=kOutput, calls=%fused_computation | convolution fusion | flops 301989888 | bytes 2359296 | tf_op jit(solution)/shard_map/dot_general | solution.py:8
  114.1 1.9 %multiply_reduce_fusion = (f32[128,2]{0,1:T(2,128)S(1)}, bf16[128,192]{0,1:T(8,128)(2,1)}) fusion(f32[128,192]{0,1:T(8,128)S(1)} %convert_element_type.47, f32[128,2]{0,1:T(2,128)S(1)} %copy-done.6, bf16[512,192,1]{1,0,2:T(8,128)(2,1)} %bitcast.8, pred[128,2,512]{2,1,0:T(4,128)(4,1)S(1)} %eq.50), kind=kOutput, calls=%fused_computation.32 | convolution fusion | flops 50503424 | bytes 477184 | tf_op jit(solution)/shard_map/dot_general | solution.py:8
  116.0 6.3 %psum.7 = f32[128,2]{0,1:T(2,128)} all-reduce(f32[128,2]{0,1:T(2,128)S(1)} %get-tuple-element.7), channel_id=1, replica_groups=mesh['node'=4,'grp'=2,'rep'=4] {'rep'}, use_global_device_ids=true, to_apply=%region_4.0 | all-reduce | flops 256 | bytes 2048 | tf_op jit(solution)/shard_map/psum | solution.py:68
  122.3 0.9 convolution_reduce_fusion
  (25 shorter events, 0.2 us)
Async XLA Ops:
  7.2 10.8 %copy-start.5 = (f32[1,384]{1,0:T(1,128)S(1)}, f32[1,384]{1,0:T(1,128)}, u32[]{:S(2)}) copy-start(f32[1,384]{1,0:T(1,128)} %param.12) | copy-start | bytes 4612
  8.2 27.4 %copy-start.3 = (bf16[1,768,384]{2,1,0:T(8,128)(2,1)S(1)}, bf16[1,768,384]{2,1,0:T(8,128)(2,1)}, u32[]{:S(2)}) copy-start(bf16[1,768,384]{2,1,0:T(8,128)(2,1)} %param.11) | copy-start | bytes 1769476
  10.6 16.2 %all-to-all-start = ((bf16[8,64,192]{2,1,0:T(8,128)(2,1)}), bf16[8,64,192]{2,1,0:T(8,128)(2,1)S(1)}, u32[]{:S(2)}, u32[]{:S(2)}) async-start(bf16[8,64,192]{2,1,0:T(8,128)(2,1)} %bitcast), calls=%async_computation | async-start | bytes 524288 | tf_op jit(solution)/shard_map/all_to_all | solution.py:20
  17.9 68.1 %all-gather.3.cloned.1.call-start = ((), (), s32[]{:S(2)}) async-start(), calls=%async_computation.6 | async-start | bytes 1966080 | tf_op jit(solution)/shard_map/all_gather | solution.py:56
  35.6 1.8 %copy-start.6 = (f32[128,2]{0,1:T(2,128)S(1)}, f32[128,2]{0,1:T(2,128)}, u32[]{:S(2)}) copy-start(f32[128,2]{0,1:T(2,128)} %param.9) | copy-start | bytes 3076
  35.6 2.1 %copy-start.4 = (bf16[128,192]{0,1:T(8,128)(2,1)S(1)}, bf16[128,192]{0,1:T(8,128)(2,1)}, u32[]{:S(2)}) copy-start(bf16[128,192]{0,1:T(8,128)(2,1)} %param.15) | copy-start | bytes 147460
  37.3 63.4 %all-gather.5.cloned.1.call-start = ((), (), s32[]{:S(2)}) async-start(), calls=%async_computation.7 | async-start | bytes 1966080 | tf_op jit(solution)/shard_map/all_gather | solution.py:88
  38.1 21.3 %copy-start.2 = (bf16[1,384,768]{2,1,0:T(8,128)(2,1)S(1)}, bf16[1,384,768]{2,1,0:T(8,128)(2,1)}, u32[]{:S(2)}) copy-start(bf16[1,384,768]{2,1,0:T(8,128)(2,1)} %param.13) | copy-start | bytes 1769476
  63.3 18.0 %all-to-all-start.1 = ((bf16[384,4,192]{0,2,1:T(8,128)(2,1)}), bf16[384,4,192]{0,2,1:T(8,128)(2,1)S(1)}, u32[]{:S(2)}, u32[]{:S(2)}) async-start(bf16[384,4,192]{0,2,1:T(8,128)(2,1)} %bitcast.3), calls=%async_computation.1 | async-start | bytes 1179648 | tf_op jit(solution)/shard_map/all_to_all | solution.py:53
  66.8 19.2 %copy-start.7 = (f32[1,192]{1,0:T(1,128)S(1)}, f32[1,192]{1,0:T(1,128)}, u32[]{:S(2)}) copy-start(f32[1,192]{1,0:T(1,128)} %param.14) | copy-start | bytes 2308
  81.3 13.0 %all-to-all-start.4 = ((bf16[4,192,384]{2,1,0:T(8,128)(2,1)}), bf16[4,192,384]{2,1,0:T(8,128)(2,1)S(1)}, u32[]{:S(2)}, u32[]{:S(2)}) async-start(bf16[4,192,384]{2,1,0:T(8,128)(2,1)} %bitcast.56), calls=%async_computation.4 | async-start | bytes 1179648 | tf_op jit(solution)/shard_map/all_to_all | solution.py:86
  86.0 13.1 %copy-start.1 = (bf16[512,384]{1,0:T(8,128)(2,1)S(1)}, bf16[512,384]{1,0:T(8,128)(2,1)}, u32[]{:S(2)}) copy-start(bf16[512,384]{1,0:T(8,128)(2,1)} %get-tuple-element.12) | copy-start | bytes 1179652
  94.3 13.5 %all-to-all-start.2 = ((bf16[8,64,192]{2,1,0:T(8,128)(2,1)}), bf16[8,64,192]{2,1,0:T(8,128)(2,1)}, u32[]{:S(2)}, u32[]{:S(2)}) async-start(bf16[8,64,192]{2,1,0:T(8,128)(2,1)} %bitcast.6), calls=%async_computation.2 | async-start | bytes 524288 | tf_op jit(solution)/shard_map/all_to_all | solution.py:20
  100.7 11.9 %copy-start = (bf16[512,384]{1,0:T(8,128)(2,1)S(1)}, bf16[512,384]{1,0:T(8,128)(2,1)}, u32[]{:S(2)}) copy-start(bf16[512,384]{1,0:T(8,128)(2,1)} %get-tuple-element.9) | copy-start | bytes 1179652
  107.8 14.5 %all-to-all-start.5 = ((bf16[8,64,192]{2,1,0:T(8,128)(2,1)}), bf16[8,64,192]{2,1,0:T(8,128)(2,1)S(1)}, u32[]{:S(2)}, u32[]{:S(2)}) async-start(bf16[8,64,192]{2,1,0:T(8,128)(2,1)} %bitcast.14), calls=%async_computation.5 | async-start | bytes 524288 | tf_op jit(solution)/shard_map/all_to_all | solution.py:20
Sparse Core Ops, SparseCore 0:
  37.5 17.8 all-gather.2
  62.3 23.7 all-gather.4
where the time goes:
time: 131 us; the launch traced here: 130 us
  blocking collectives  35.6 us (27%)
  waiting for transfers between devices  32.7 us (25%)
  starting transfers between devices  22.7 us (17%)
  matrix products  15.4 us (12%)
  between operations  14.3 us (11%)
  local copies, waits for them, and re-layouts  8.35 us (6%)
    all_to_all x3, starting transfers between devices, relocate(): lax.all_to_all(buffer, ('node', 'grp'), split_axis=0, concat_axis=0, tile...  15.7 us
    all_to_all x1, waiting for transfers between devices, per_device(): lax.all_to_all(w_second, 'rep', split_axis=1, concat_axis=0, tiled=True)  14.5 us
    all_to_all x3, waiting for transfers between devices, relocate(): lax.all_to_all(buffer, ('node', 'grp'), split_axis=0, concat_axis=0, tile...  12.9 us
    all_to_all x1, blocking collectives, relocate(): lax.all_to_all(buffer, ('node', 'grp'), split_axis=0, concat_axis=0, tile...  12.8 us
    all_gather x1, blocking collectives, per_device(): full_x = lax.all_gather(expert_x, 'rep', axis=1, tiled=True)  8.6 us
    all_gather x1, blocking collectives, per_device(): full_grad = lax.all_gather(expert_grad, 'rep', axis=1, tiled=True)  7.84 us
    psum x1, blocking collectives, per_device(): d_gates = lax.psum(gate_terms, 'rep')  6.32 us
    dot_general x4, matrix products, contract_first(): lax.dot_general(left, right, (((0,), (0,)), ((), ())), preferred_element_...  5.86 us
  transfers between devices with their start and end apart: 7, of which 4 were waited for; matrix products, arithmetic and copies ran while one was open for 14% of the time, Pallas kernels for 0%

commit v1 on v0

--- a/solution.py
+++ b/solution.py
@@ -50,7 +50,9 @@
     pre_act = jnp.dot(full_x, w_first, preferred_element_type=jnp.float32)
     pre_act = pre_act + bias_first
     hidden = jax.nn.gelu(pre_act).astype(jnp.bfloat16)
-    second_block = lax.all_to_all(w_second, "rep", split_axis=1, concat_axis=0, tiled=True)
+    shards = jnp.split(w_second, lax.axis_size("rep"), axis=1)
+    arrived = lax.all_to_all(jnp.stack(shards), "rep", 0, 0)
+    second_block = jnp.concatenate(arrived, axis=0)
     weights = second_block
     summed = jnp.dot(
         lax.all_gather(hidden, "rep", axis=1, tiled=True),

time: 131 us -> 131 us (level)
  no operation moved by 1% of the time
where the time goes in v1:
time: 131 us; the launch traced here: 130 us
  blocking collectives  35.6 us (27%)
  waiting for transfers between devices  32.9 us (25%)
  starting transfers between devices  22.7 us (17%)
  matrix products  15.4 us (12%)
  between operations  14.3 us (11%)
  local copies, waits for them, and re-layouts  7.66 us (6%)
  other arithmetic  1.93 us (1%)
    all_to_all x3, starting transfers between devices, relocate(): lax.all_to_all(buffer, ('node', 'grp'), split_axis=0, concat_axis=0, tile...  15.7 us
    all_to_all x1, waiting for transfers between devices, per_device(): arrived = lax.all_to_all(jnp.stack(shards), 'rep', 0, 0)  14.7 us
    all_to_all x3, waiting for transfers between devices, relocate(): lax.all_to_all(buffer, ('node', 'grp'), split_axis=0, concat_axis=0, tile...  12.9 us
    all_to_all x1, blocking collectives, relocate(): lax.all_to_all(buffer, ('node', 'grp'), split_axis=0, concat_axis=0, tile...  12.8 us
    all_gather x1, blocking collectives, per_device(): full_x = lax.all_gather(expert_x, 'rep', axis=1, tiled=True)  8.6 us
    all_gather x1, blocking collectives, per_device(): full_grad = lax.all_gather(expert_grad, 'rep', axis=1, tiled=True)  7.84 us
    psum x1, blocking collectives, per_device(): d_gates = lax.psum(gate_terms, 'rep')  6.32 us
    dot_general x4, matrix products, contract_first(): lax.dot_general(left, right, (((0,), (0,)), ((), ())), preferred_element_...  5.86 us
  transfers between devices with their start and end apart: 7, of which 4 were waited for; matrix products, arithmetic and copies ran while one was open for 14% of the time, Pallas kernels for 0%

profile of v1, /device:TPU:0, one launch (start us, length us, event | category | flops | bytes accessed | tf_op | source)
XLA Modules:
  0.0 130.5 jit_solution(5463202274089670900)
XLA Ops:
  7.2 0.9 copy.63
  8.1 0.1 broadcast_in_dim.10
  8.2 0.1 reshape.107
  8.3 0.8 copy.62
  9.1 0.1 reshape.106
  9.3 0.2 convert_reduce_fusion.2
  9.5 0.3 convolution_convert_fusion.2
  9.8 0.8 copy.64
  10.6 7.3 %all-to-all-start = ((bf16[8,64,192]{2,1,0:T(8,128)(2,1)}), bf16[8,64,192]{2,1,0:T(8,128)(2,1)S(1)}, u32[]{:S(2)}, u32[]{:S(2)}) async-start(bf16[8,64,192]{2,1,0:T(8,128)(2,1)} %bitcast), calls=%async_computation | async-start | bytes 524288 | tf_op jit(solution)/shard_map/all_to_all | solution.py:20
  18.0 8.8 %all-to-all-done = bf16[8,64,192]{2,1,0:T(8,128)(2,1)S(1)} async-done(((bf16[8,64,192]{2,1,0:T(8,128)(2,1)}), bf16[8,64,192]{2,1,0:T(8,128)(2,1)S(1)}, u32[]{:S(2)}, u32[]{:S(2)}) %all-to-all-start) | async-done | bytes 196640 | tf_op jit(solution)/shard_map/all_to_all | solution.py:20
  26.8 0.1 copy.65
  27.0 8.6 %all_gather.12 = bf16[512,768]{0,1:T(8,128)(2,1)S(1)} all-gather(bf16[512,192]{0,1:T(8,128)(2,1)S(1)} %copy.65), channel_id=1, replica_groups=mesh['node'=4,'grp'=2,'rep'=4] {'rep'}, dimensions={1}, use_global_device_ids=true | all-gather | bytes 983040 | tf_op jit(solution)/shard_map/all_gather | solution.py:49
  35.6 1.8 %multiply_convert_fusion = (bf16[512,384]{1,0:T(8,128)(2,1)}, f32[512,384]{1,0:T(8,128)}) fusion(f32[384]{0:T(512)S(1)} %reduce.1, bf16[512,768]{0,1:T(8,128)(2,1)S(1)} %all_gather.12, bf16[1,768,384]{2,1,0:T(8,128)(2,1)S(1)} %copy-done.3), kind=kOutput, calls=%fused_computation.19 | convolution fusion | flops 303955968 | bytes 2557440 | tf_op jit(solution)/shard_map/dot_general | solution.py:50
  37.4 0.1 copy.71
  37.5 0.1 mul.97
  37.7 0.1 copy.83
  37.8 0.1 mul.99.clone
  37.9 0.2 mul.100
  38.1 0.3 convolution_convert_fusion.1
  38.4 0.1 copy.73
  38.5 12.8 %all_to_all.44 = bf16[8,64,192]{2,1,0:T(8,128)(2,1)S(1)} all-to-all(bf16[8,64,192]{2,1,0:T(8,128)(2,1)S(1)} %bitcast.63), channel_id=1, replica_groups=mesh['node'=4,'grp'=2,'rep'=4] {'node','grp'}, dimensions={0} | all-to-all | bytes 393216 | tf_op jit(solution)/shard_map/all_to_all | solution.py:20
  51.4 0.1 copy.74
  51.5 7.8 %all_gather.14 = bf16[512,768]{0,1:T(8,128)(2,1)S(1)} all-gather(bf16[512,192]{0,1:T(8,128)(2,1)S(1)} %copy.74), channel_id=1, replica_groups=mesh['node'=4,'grp'=2,'rep'=4] {'rep'}, dimensions={1}, use_global_device_ids=true | all-gather | bytes 983040 | tf_op jit(solution)/shard_map/all_gather | solution.py:81
  59.3 2.9 %convert_reduce_fusion = (f32[384]{0:T(512)S(1)}, bf16[512,384]{1,0:T(8,128)(2,1)}) fusion(f32[512,384]{1,0:T(8,128)} %get-tuple-element.14, bf16[512,768]{0,1:T(8,128)(2,1)S(1)} %all_gather.14, bf16[1,384,768]{2,1,0:T(8,128)(2,1)S(1)} %copy-done.2), kind=kOutput, calls=%fused_computation.18 | convolution fusion | flops 306314880 | bytes 2557440 | tf_op jit(solution)/shard_map/dot_general | solution.py:14
  62.2 0.3 copy.66
  62.5 0.1 slice_bitcast_fusion.3
  62.6 0.9 pad_maximum_fusion
  63.5 3.5 %all-to-all-start.1 = ((bf16[4,384,192]{1,2,0:T(8,128)(2,1)}), bf16[4,384,192]{1,2,0:T(8,128)(2,1)S(1)}, u32[]{:S(2)}, u32[]{:S(2)}) async-start(bf16[4,384,192]{1,2,0:T(8,128)(2,1)} %pad_maximum_fusion), calls=%async_computation.1 | async-start | bytes 1179648 | tf_op jit(solution)/shard_map/all_to_all | solution.py:54
  67.0 14.7 %all-to-all-done.1 = bf16[4,384,192]{1,2,0:T(8,128)(2,1)S(1)} async-done(((bf16[4,384,192]{1,2,0:T(8,128)(2,1)}), bf16[4,384,192]{1,2,0:T(8,128)(2,1)S(1)}, u32[]{:S(2)}, u32[]{:S(2)}) %all-to-all-start.1) | async-done | bytes 589856 | tf_op jit(solution)/shard_map/all_to_all | solution.py:54
  81.8 3.5 %all-to-all-start.4 = ((bf16[4,192,384]{2,1,0:T(8,128)(2,1)}), bf16[4,192,384]{2,1,0:T(8,128)(2,1)S(1)}, u32[]{:S(2)}, u32[]{:S(2)}) async-start(bf16[4,192,384]{2,1,0:T(8,128)(2,1)} %bitcast.64), calls=%async_computation.4 | async-start | bytes 1179648 | tf_op jit(solution)/shard_map/all_to_all | solution.py:88
  85.2 0.1 iota_compare_fusion.3
  85.4 0.2 eq.50
  85.6 0.9 copy.84
  86.4 2.2 %fusion = bf16[512,192]{0,1:T(8,128)(2,1)S(1)} fusion(bf16[512,1536]{1,0:T(8,128)(2,1)} %all-gather.3.cloned.1.call-done, bf16[1536,192]{0,1:T(8,128)(2,1)} %bitcast.66, f32[192]{0:T(256)S(1)} %bitcast.69), kind=kOutput, calls=%fused_computation.5 | convolution fusion | flops 302186496 | bytes 2360064 | tf_op jit(solution)/shard_map/dot_general | solution.py:57
  88.7 0.8 copy.68
  89.5 5.2 %all-to-all-done.4 = bf16[4,192,384]{2,1,0:T(8,128)(2,1)S(1)} async-done(((bf16[4,192,384]{2,1,0:T(8,128)(2,1)}), bf16[4,192,384]{2,1,0:T(8,128)(2,1)S(1)}, u32[]{:S(2)}, u32[]{:S(2)}) %all-to-all-start.4) | async-done | bytes 589856 | tf_op jit(solution)/shard_map/all_to_all | solution.py:88
  94.7 4.8 %all-to-all-start.2 = ((bf16[8,64,192]{2,1,0:T(8,128)(2,1)}), bf16[8,64,192]{2,1,0:T(8,128)(2,1)}, u32[]{:S(2)}, u32[]{:S(2)}) async-start(bf16[8,64,192]{2,1,0:T(8,128)(2,1)} %bitcast.9), calls=%async_computation.2 | async-start | bytes 524288 | tf_op jit(solution)/shard_map/all_to_all | solution.py:20
  99.5 1.6 %convolution_bitcast_fusion.1 = f32[1,768,384]{2,1,0:T(8,128)} fusion(bf16[512,768]{0,1:T(8,128)(2,1)S(1)} %all_gather.12, bf16[512,384]{1,0:T(8,128)(2,1)S(1)} %copy-done.1), kind=kOutput, calls=%fused_computation.1 | convolution fusion | flops 301989888 | bytes 2359296 | tf_op jit(solution)/shard_map/dot_general | solution.py:8
  101.2 2.1 %convolution_convert_fusion = bf16[512,192]{0,1:T(8,128)(2,1)S(1)} fusion(bf16[512,1536]{1,0:T(8,128)(2,1)} %all-gather.5.cloned.1.call-done, bf16[192,1536]{1,0:T(8,128)(2,1)S(1)} %bitcast.65), kind=kOutput, calls=%fused_computation.4 | convolution fusion | flops 302088192 | bytes 2359296 | tf_op jit(solution)/shard_map/dot_general | solution.py:14
  103.3 0.8 copy.76
  104.2 4.1 %all-to-all-done.2 = bf16[8,64,192]{2,1,0:T(8,128)(2,1)} async-done(((bf16[8,64,192]{2,1,0:T(8,128)(2,1)}), bf16[8,64,192]{2,1,0:T(8,128)(2,1)}, u32[]{:S(2)}, u32[]{:S(2)}) %all-to-all-start.2) | async-done | bytes 196640 | tf_op jit(solution)/shard_map/all_to_all | solution.py:20
  108.2 3.6 %all-to-all-start.5 = ((bf16[8,64,192]{2,1,0:T(8,128)(2,1)}), bf16[8,64,192]{2,1,0:T(8,128)(2,1)S(1)}, u32[]{:S(2)}, u32[]{:S(2)}) async-start(bf16[8,64,192]{2,1,0:T(8,128)(2,1)} %bitcast.16), calls=%async_computation.5 | async-start | bytes 524288 | tf_op jit(solution)/shard_map/all_to_all | solution.py:20
  111.8 0.7 convert_reduce_fusion.1
  112.5 0.6 broadcast_in_dim.12
  113.0 1.5 %convolution_bitcast_fusion = f32[1,384,768]{2,1,0:T(8,128)} fusion(bf16[512,384]{1,0:T(8,128)(2,1)S(1)} %copy-done, bf16[512,768]{0,1:T(8,128)(2,1)S(1)} %all_gather.14), kind=kOutput, calls=%fused_computation | convolution fusion | flops 301989888 | bytes 2359296 | tf_op jit(solution)/shard_map/dot_general | solution.py:8
  114.6 1.9 %multiply_reduce_fusion = (f32[128,2]{0,1:T(2,128)S(1)}, bf16[128,192]{0,1:T(8,128)(2,1)}) fusion(f32[128,192]{0,1:T(8,128)S(1)} %convert_element_type.47, f32[128,2]{0,1:T(2,128)S(1)} %copy-done.6, bf16[512,192,1]{1,0,2:T(8,128)(2,1)} %bitcast.11, pred[128,2,512]{2,1,0:T(4,128)(4,1)S(1)} %eq.50), kind=kOutput, calls=%fused_computation.33 | convolution fusion | flops 50503424 | bytes 477184 | tf_op jit(solution)/shard_map/dot_general | solution.py:8
  116.4 6.3 %psum.7 = f32[128,2]{0,1:T(2,128)} all-reduce(f32[128,2]{0,1:T(2,128)S(1)} %get-tuple-element.7), channel_id=1, replica_groups=mesh['node'=4,'grp'=2,'rep'=4] {'rep'}, use_global_device_ids=true, to_apply=%region_4.0 | all-reduce | flops 256 | bytes 2048 | tf_op jit(solution)/shard_map/psum | solution.py:70
  122.7 0.9 convolution_reduce_fusion
  (27 shorter events, 0.3 us)
Async XLA Ops:
  7.2 10.8 %copy-start.5 = (f32[1,384]{1,0:T(1,128)S(1)}, f32[1,384]{1,0:T(1,128)}, u32[]{:S(2)}) copy-start(f32[1,384]{1,0:T(1,128)} %param.12) | copy-start | bytes 4612
  8.2 27.4 %copy-start.3 = (bf16[1,768,384]{2,1,0:T(8,128)(2,1)S(1)}, bf16[1,768,384]{2,1,0:T(8,128)(2,1)}, u32[]{:S(2)}) copy-start(bf16[1,768,384]{2,1,0:T(8,128)(2,1)} %param.11) | copy-start | bytes 1769476
  10.6 16.2 %all-to-all-start = ((bf16[8,64,192]{2,1,0:T(8,128)(2,1)}), bf16[8,64,192]{2,1,0:T(8,128)(2,1)S(1)}, u32[]{:S(2)}, u32[]{:S(2)}) async-start(bf16[8,64,192]{2,1,0:T(8,128)(2,1)} %bitcast), calls=%async_computation | async-start | bytes 524288 | tf_op jit(solution)/shard_map/all_to_all | solution.py:20
  17.9 68.5 %all-gather.3.cloned.1.call-start = ((), (), s32[]{:S(2)}) async-start(), calls=%async_computation.6 | async-start | bytes 1966080 | tf_op jit(solution)/shard_map/all_gather | solution.py:58
  35.6 1.8 %copy-start.6 = (f32[128,2]{0,1:T(2,128)S(1)}, f32[128,2]{0,1:T(2,128)}, u32[]{:S(2)}) copy-start(f32[128,2]{0,1:T(2,128)} %param.9) | copy-start | bytes 3076
  35.6 2.1 %copy-start.4 = (bf16[128,192]{0,1:T(8,128)(2,1)S(1)}, bf16[128,192]{0,1:T(8,128)(2,1)}, u32[]{:S(2)}) copy-start(bf16[128,192]{0,1:T(8,128)(2,1)} %param.15) | copy-start | bytes 147460
  37.3 63.8 %all-gather.5.cloned.1.call-start = ((), (), s32[]{:S(2)}) async-start(), calls=%async_computation.7 | async-start | bytes 1966080 | tf_op jit(solution)/shard_map/all_gather | solution.py:90
  38.1 21.3 %copy-start.2 = (bf16[1,384,768]{2,1,0:T(8,128)(2,1)S(1)}, bf16[1,384,768]{2,1,0:T(8,128)(2,1)}, u32[]{:S(2)}) copy-start(bf16[1,384,768]{2,1,0:T(8,128)(2,1)} %param.13) | copy-start | bytes 1769476
  63.5 18.3 %all-to-all-start.1 = ((bf16[4,384,192]{1,2,0:T(8,128)(2,1)}), bf16[4,384,192]{1,2,0:T(8,128)(2,1)S(1)}, u32[]{:S(2)}, u32[]{:S(2)}) async-start(bf16[4,384,192]{1,2,0:T(8,128)(2,1)} %pad_maximum_fusion), calls=%async_computation.1 | async-start | bytes 1179648 | tf_op jit(solution)/shard_map/all_to_all | solution.py:54
  67.0 19.5 %copy-start.7 = (f32[1,192]{1,0:T(1,128)S(1)}, f32[1,192]{1,0:T(1,128)}, u32[]{:S(2)}) copy-start(f32[1,192]{1,0:T(1,128)} %param.14) | copy-start | bytes 2308
  81.8 13.0 %all-to-all-start.4 = ((bf16[4,192,384]{2,1,0:T(8,128)(2,1)}), bf16[4,192,384]{2,1,0:T(8,128)(2,1)S(1)}, u32[]{:S(2)}, u32[]{:S(2)}) async-start(bf16[4,192,384]{2,1,0:T(8,128)(2,1)} %bitcast.64), calls=%async_computation.4 | async-start | bytes 1179648 | tf_op jit(solution)/shard_map/all_to_all | solution.py:88
  86.4 13.1 %copy-start.1 = (bf16[512,384]{1,0:T(8,128)(2,1)S(1)}, bf16[512,384]{1,0:T(8,128)(2,1)}, u32[]{:S(2)}) copy-start(bf16[512,384]{1,0:T(8,128)(2,1)} %get-tuple-element.16) | copy-start | bytes 1179652
  94.7 13.5 %all-to-all-start.2 = ((bf16[8,64,192]{2,1,0:T(8,128)(2,1)}), bf16[8,64,192]{2,1,0:T(8,128)(2,1)}, u32[]{:S(2)}, u32[]{:S(2)}) async-start(bf16[8,64,192]{2,1,0:T(8,128)(2,1)} %bitcast.9), calls=%async_computation.2 | async-start | bytes 524288 | tf_op jit(solution)/shard_map/all_to_all | solution.py:20
  101.2 11.9 %copy-start = (bf16[512,384]{1,0:T(8,128)(2,1)S(1)}, bf16[512,384]{1,0:T(8,128)(2,1)}, u32[]{:S(2)}) copy-start(bf16[512,384]{1,0:T(8,128)(2,1)} %get-tuple-element.13) | copy-start | bytes 1179652
  108.2 14.5 %all-to-all-start.5 = ((bf16[8,64,192]{2,1,0:T(8,128)(2,1)}), bf16[8,64,192]{2,1,0:T(8,128)(2,1)S(1)}, u32[]{:S(2)}, u32[]{:S(2)}) async-start(bf16[8,64,192]{2,1,0:T(8,128)(2,1)} %bitcast.16), calls=%async_computation.5 | async-start | bytes 524288 | tf_op jit(solution)/shard_map/all_to_all | solution.py:20
Sparse Core Ops, SparseCore 0:
  37.5 17.8 all-gather.2
  62.3 24.0 all-gather.4
